TPU v7x, 32 devices: a whole 2x2x4 slice. The times are simulated.
32 devices in a mesh: leaf: 2 (over core), row: 4 (over y, x), col: 4 (over z).
Axes of the slice: x: 2, y: 2, z: 4, core: 2. Of those that a mesh axis runs over, the one named last changes fastest.
Arguments:
- rhs_leaf: bfloat16 [2, 8, 64, 2048], P('leaf', None, None, 'col'), may hold values from -6 to 6
- dinv_leaf: bfloat16 [2, 8, 2048, 2048], P('leaf', None, 'row', 'col'), as said below
- panel_leaf: bfloat16 [2, 8, 1024, 2048], P('leaf', None, 'col', 'row'), may hold values from -0.0625 to 0.0625
- counts: int32 [2, 8], P('leaf'), may hold values from 256 to 2048, as said below
- row_index: int32 [2, 8, 1024], P('leaf'), may hold values from 0 to 4095, as said below
- rhs_root: bfloat16 [64, 4096], P(None, 'col'), may hold values from -6 to 6
- dinv_root: bfloat16 [4096, 4096], P(('leaf', 'row')), as said below
Outputs:
- y_leaf: bfloat16 [2, 8, 64, 2048], P('leaf', None, None, 'row')
- y_root: bfloat16 [64, 4096], P(None, ('leaf', 'row'))
Inputs may be any that keep to these rules, and one draw needn't show every extreme that they name: `counts`: each subtree supernode has at least 256 columns; at least one supernode of every draw has all 2048. `row_index`: within one supernode the 1024 entries are distinct and increasing. `dinv_leaf`: each [2048, 2048] block is lower triangular with a nonzero diagonal. `dinv_root`: lower triangular with a nonzero diagonal.
All inputs are finite; a program needn't handle non-finite values.
Results may differ from a plain program's by a relative error of at most 0.0053.
Values may be sent and summed in bfloat16 or wider, within the bound.
No kernel may reach another device: no remote copies, remote signals or barrier semaphores. Data moves between devices by JAX's collectives and lax.ppermute only.
A program may use at most 64 MiB of HBM per device.

v0:
```python
import jax
import jax.numpy as jnp
from jax import lax
from jax.sharding import PartitionSpec as P


def local(rhs_leaf, dinv_leaf, panel_leaf, counts, row_index, rhs_root, dinv_root):
    width_col = rhs_leaf.shape[3]
    width_row = dinv_leaf.shape[2]
    panel_rows = panel_leaf.shape[2]
    columns = rhs_root.shape[0]
    sep_width = rhs_root.shape[1] * lax.axis_size("col")
    limit = counts[0][:, None, None]
    col_slots = lax.axis_index("col") * width_col + lax.iota(jnp.int32, width_col)
    masked = jnp.where(col_slots[None, None, :] < limit, rhs_leaf[0], jnp.zeros((), jnp.bfloat16))
    partial_value = jnp.einsum(
        "kbj,kij->kbi", masked, dinv_leaf[0], preferred_element_type=jnp.float32
    )
    summed = lax.psum(partial_value, "col")
    row_slots = lax.axis_index("row") * width_row + lax.iota(jnp.int32, width_row)
    live_rows = (row_slots[None, None, :] < limit).astype(jnp.float32)
    solved = (summed * live_rows).astype(jnp.bfloat16)
    update = jnp.einsum("kbi,kri->kbr", solved, panel_leaf[0], preferred_element_type=jnp.float32)
    offset = lax.axis_index("col") * panel_rows
    targets = lax.dynamic_slice_in_dim(row_index[0], offset, panel_rows, 1)
    flat_update = jnp.transpose(update, (1, 0, 2)).reshape(columns, -1)
    accum = jnp.zeros((columns, sep_width), jnp.float32).at[:, targets.reshape(-1)].add(flat_update)
    piece = lax.psum_scatter(accum, "col", scatter_dimension=1, tiled=True)
    share = lax.psum(piece, ("leaf", "row"))
    reduced = (rhs_root.astype(jnp.float32) - share).astype(jnp.bfloat16)
    whole_reduced = lax.all_gather(reduced, "col", axis=1, tiled=True)
    y_root = jnp.dot(whole_reduced, dinv_root.T, preferred_element_type=jnp.float32).astype(
        jnp.bfloat16
    )
    return (solved[None], y_root)


def solution(mesh):
    in_specs = (
        P("leaf", None, None, "col"),
        P("leaf", None, "row", "col"),
        P("leaf", None, "col", "row"),
        P("leaf", None),
        P("leaf", None, None),
        P(None, "col"),
        P(("leaf", "row"), None),
    )
    out_specs = (P("leaf", None, None, "row"), P(None, ("leaf", "row")))
    return jax.shard_map(local, mesh=mesh, in_specs=in_specs, out_specs=out_specs, check_vma=False)
```

profile of v0, /device:TPU:0, one launch (start us, length us, event | category | flops | bytes accessed | tf_op | source)
XLA Modules:
  0.0 218.8 jit_solution(5079778243573968000)
XLA Ops:
  7.2 0.0 copy-start
  7.2 0.0 all-reduce.3.cloned.1.call-start
  7.2 0.9 compare_convert_fusion
  8.1 4.7 %fusion = f32[8,64,512]{2,1,0:T(8,128)} fusion(bf16[1,8,512,512]{3,2,1,0:T(8,128)(2,1)} %param.8, bf16[1,8,64,512]{3,2,1,0:T(8,128)(2,1)} %param.7, pred[8,512]{1,0:T(8,128)(4,1)S(1)} %get-tuple-element.3), kind=kOutput, calls=%fused_computation.1 | convolution fusion | flops 268697600 | bytes 5771264 | tf_op jit(solution)/shard_map/kbj,kij->kbi/dot_general | solution.py:16
  12.8 0.0 all-reduce.3.cloned.1.call-update
  12.8 0.0 reduce-scatter.2.cloned.1.call-start
  12.9 0.7 dynamic-slice_bitcast_fusion
  13.6 54.0 %all-reduce.3.cloned.1.call-done = f32[8,64,512]{2,1,0:T(8,128)} async-done(((f32[8,64,512]{2,1,0:T(8,128)}), f32[8,64,512]{2,1,0:T(8,128)}) %all-reduce.3.cloned.1.call-update) | async-done | bytes 1048592 | tf_op jit(solution)/shard_map/psum | solution.py:19
  67.6 0.0 copy-done
  67.6 2.0 fusion.4
  69.6 0.1 copy.13
  69.7 1.3 copy.12
  71.0 13.3 %scatter_custom_fusion = f32[64,4096]{0,1:T(8,128)} fusion(s32[2048]{0:T(1024)S(1)} %bitcast.29, f32[2048,64]{1,0:T(8,128)} %copy.12, f32[]{:T(128)} %constant.7.clone.1), kind=kCustom, calls=%fused_computation.7 | custom fusion | flops 131072 | bytes 1049088 | tf_op jit(solution)/shard_map/scatter-add | solution.py:27
  84.3 0.0 reduce-scatter.2.cloned.1.call-update
  84.3 0.0 all-reduce.5.cloned.1.call-start
  84.4 0.0 copy-done.2
  84.4 0.2 copy.10
  84.6 42.8 %reduce-scatter.2.cloned.1.call-done = f32[64,1024]{0,1:T(8,128)} async-done(((f32[64,4096]{0,1:T(8,128)}), f32[64,1024]{0,1:T(8,128)}) %reduce-scatter.2.cloned.1.call-update) | async-done | bytes 262160 | tf_op jit(solution)/shard_map/reduce_scatter | solution.py:28
  127.4 0.0 all-reduce.5.cloned.1.call-update
  127.4 0.9 fusion.11
  128.4 56.2 %all-reduce.5.cloned.1.call-done = f32[64,1024]{0,1:T(8,128)} async-done(((f32[64,1024]{0,1:T(8,128)}), f32[64,1024]{0,1:T(8,128)}) %all-reduce.5.cloned.1.call-update) | async-done | bytes 262160 | tf_op jit(solution)/shard_map/psum | solution.py:29
  184.5 1.1 subtract_convert_fusion
  185.6 22.4 %all_gather.3 = bf16[64,4096]{0,1:T(8,128)(2,1)S(1)} all-gather(bf16[64,1024]{0,1:T(8,128)(2,1)S(1)} %subtract_convert_fusion), channel_id=1, replica_groups=mesh['leaf'=2,'row'=4,'col'=4] {'col'}, dimensions={1}, use_global_device_ids=true | all-gather | bytes 655360 | tf_op jit(solution)/shard_map/all_gather | solution.py:31
  208.0 4.2 %convolution_convert_fusion = bf16[64,512]{1,0:T(8,128)(2,1)} fusion(bf16[64,4096]{0,1:T(8,128)(2,1)S(1)} %all_gather.3, bf16[512,4096]{1,0:T(8,128)(2,1)} %param.13), kind=kOutput, calls=%fused_computation.6 | convolution fusion | flops 268468224 | bytes 4784128 | tf_op jit(solution)/shard_map/dot_general | solution.py:32
  (6 shorter events, 0.0 us)
Async XLA Ops:
  7.2 60.5 %copy-start = (bf16[1,8,256,512]{3,2,1,0:T(8,128)(2,1)S(1)}, bf16[1,8,256,512]{3,2,1,0:T(8,128)(2,1)}, u32[]{:S(2)}) copy-start(bf16[1,8,256,512]{3,2,1,0:T(8,128)(2,1)} %param.9) | copy-start | bytes 6291460
  7.2 60.4 %all-reduce.3.cloned.1.call-start = ((), (), s32[]{:S(2)}) async-start(), calls=%async_computation.1 | async-start | bytes 2097152 | tf_op jit(solution)/shard_map/psum | solution.py:19
  12.8 114.6 %reduce-scatter.2.cloned.1.call-start = ((), (), s32[]{:S(2)}) async-start(), calls=%async_computation.2 | async-start | bytes 2621440 | tf_op jit(solution)/shard_map/reduce_scatter | solution.py:28
  71.0 13.4 %copy-start.2 = (bf16[64,1024]{1,0:T(8,128)(2,1)S(1)}, bf16[64,1024]{1,0:T(8,128)(2,1)}, u32[]{:S(2)}) copy-start(bf16[64,1024]{1,0:T(8,128)(2,1)} %param.12) | copy-start | bytes 393220
  71.0 56.5 %copy-start.1 = (f32[8,64,512]{2,1,0:T(8,128)S(1)}, f32[8,64,512]{2,1,0:T(8,128)}, u32[]{:S(2)}) copy-start(f32[8,64,512]{2,1,0:T(8,128)} %all-reduce.3.cloned.1.call-done) | copy-start | bytes 3145732
  84.3 100.2 %all-reduce.5.cloned.1.call-start = ((), (), s32[]{:S(2)}) async-start(), calls=%async_computation.3 | async-start | bytes 1048576 | tf_op jit(solution)/shard_map/psum | solution.py:29
Sparse Core Ops, SparseCore 0:
  13.0 54.6 all-reduce.2
  84.5 42.8 reduce-scatter.1
  130.5 53.9 all-reduce.4
where the time goes:
time: 219 us
  waiting for transfers between devices  153 us (70%)
  blocking collectives  22.4 us (10%)
  other arithmetic  16.2 us (7%)
  between operations  13.8 us (6%)
  matrix products  10.9 us (5%)
  local copies, waits for them, and re-layouts  2.27 us (1%)
    psum x1, waiting for transfers between devices, local(): share = lax.psum(piece, ('leaf', 'row'))  56.2 us
    psum x1, waiting for transfers between devices, local(): summed = lax.psum(partial_value, 'col')  54 us
    reduce_scatter x1, waiting for transfers between devices, local(): piece = lax.psum_scatter(accum, 'col', scatter_dimension=1, tiled=True)  42.8 us
    all_gather x1, blocking collectives, local(): whole_reduced = lax.all_gather(reduced, 'col', axis=1, tiled=True)  22.4 us
    scatter-add x1, other arithmetic, local(): jnp.zeros((columns, sep_width), jnp.float32).at[:, targets.reshape(-1)]  13.3 us
    dot_general x1, matrix products, local(): jnp.einsum('kbj,kij->kbi', masked, dinv_leaf[0], preferred_element_type=j...  4.71 us
  transfers between devices with their start and end apart: 3, of which 3 were waited for; matrix products, arithmetic and copies ran while one was open for 1% of the time, Pallas kernels for 0%

commit v1 on v0

--- a/solution.py
+++ b/solution.py
@@ -28,7 +28,9 @@
     piece = lax.psum_scatter(accum, "col", scatter_dimension=1, tiled=True)
     share = lax.psum(piece, ("leaf", "row"))
     reduced = (rhs_root.astype(jnp.float32) - share).astype(jnp.bfloat16)
-    whole_reduced = lax.all_gather(reduced, "col", axis=1, tiled=True)
+    whole_reduced = jnp.concatenate(
+        lax.all_to_all(jnp.stack([reduced] * lax.axis_size("col")), "col", 0, 0), axis=1
+    )
     y_root = jnp.dot(whole_reduced, dinv_root.T, preferred_element_type=jnp.float32).astype(
         jnp.bfloat16
     )

time: 219 us -> 202 us (0.922)
  blocking collectives: 22.4 us -> 0 us
  local copies, waits for them, and re-layouts: 2.27 us -> 7.24 us
  starting transfers between devices: 0.12 us -> 4.72 us
  waiting for transfers between devices: 153 us -> 149 us
    all_gather x1 -> x0, blocking collectives: 22.4 us -> none  [local(): whole_reduced = lax.all_gather(reduced, 'col', axis=1, tiled=True)]
    reduce_scatter x1, waiting for transfers between devices: 42.8 us -> 26.7 us  [local(): piece = lax.psum_scatter(accum, 'col', scatter_dimension=1, tiled=True)]
    all_to_all x0 -> x1, waiting for transfers between devices: none -> 12.9 us  [local(): lax.all_to_all(jnp.stack([reduced] * lax.axis_size('col')), 'col', 0, 0)]
    all_to_all x0 -> x1, starting transfers between devices: none -> 4.6 us  [local(): lax.all_to_all(jnp.stack([reduced] * lax.axis_size('col')), 'col', 0, 0)]
    scatter-add x0 -> x1, local copies, waits for them, and re-layouts: none -> 3.2 us  [local(): jnp.zeros((columns, sep_width), jnp.float32).at[:, targets.reshape(-1)]]
  transfers between devices with their start and end apart: 3 -> 4, of which waited for: 3 -> 4; matrix products, arithmetic and copies ran while one was open for 1% -> 1% of each run, Pallas kernels for 0% -> 0%
where the time goes in v1:
time: 202 us
  waiting for transfers between devices  149 us (74%)
  other arithmetic  16 us (8%)
  between operations  13.8 us (7%)
  matrix products  10.9 us (5%)
  local copies, waits for them, and re-layouts  7.24 us (4%)
  starting transfers between devices  4.72 us (2%)
    psum x1, waiting for transfers between devices, local(): share = lax.psum(piece, ('leaf', 'row'))  55.4 us
    psum x1, waiting for transfers between devices, local(): summed = lax.psum(partial_value, 'col')  54 us
    reduce_scatter x1, waiting for transfers between devices, local(): piece = lax.psum_scatter(accum, 'col', scatter_dimension=1, tiled=True)  26.7 us
    scatter-add x1, other arithmetic, local(): jnp.zeros((columns, sep_width), jnp.float32).at[:, targets.reshape(-1)]  13.2 us
    all_to_all x1, waiting for transfers between devices, local(): lax.all_to_all(jnp.stack([reduced] * lax.axis_size('col')), 'col', 0, 0)  12.9 us
    dot_general x1, matrix products, local(): jnp.einsum('kbj,kij->kbi', masked, dinv_leaf[0], preferred_element_type=j...  4.7 us
    all_to_all x1, starting transfers between devices, local(): lax.all_to_all(jnp.stack([reduced] * lax.axis_size('col')), 'col', 0, 0)  4.6 us
    dot_general x1, matrix products, local(): jnp.dot(whole_reduced, dinv_root.T, preferred_element_type=jnp.float32)  4.23 us
  transfers between devices with their start and end apart: 4, of which 4 were waited for; matrix products, arithmetic and copies ran while one was open for 1% of the time, Pallas kernels for 0%

profile of v1, /device:TPU:0, one launch (start us, length us, event | category | flops | bytes accessed | tf_op | source)
XLA Modules:
  0.0 201.7 jit_solution(159280099886812826)
XLA Ops:
  7.2 0.0 all-reduce.3.cloned.1.call-start
  7.2 0.9 compare_convert_fusion
  8.1 4.7 %fusion = f32[8,64,512]{2,1,0:T(8,128)} fusion(bf16[1,8,512,512]{3,2,1,0:T(8,128)(2,1)} %param.8, bf16[1,8,64,512]{3,2,1,0:T(8,128)(2,1)} %param.7, pred[8,512]{1,0:T(8,128)(4,1)S(1)} %get-tuple-element.3), kind=kOutput, calls=%fused_computation.1 | convolution fusion | flops 268697600 | bytes 5771264 | tf_op jit(solution)/shard_map/kbj,kij->kbi/dot_general | solution.py:16
  12.8 0.0 all-reduce.3.cloned.1.call-update
  12.8 0.0 reduce-scatter.2.cloned.1.call-start
  12.9 0.7 dynamic-slice_bitcast_fusion
  13.6 54.0 %all-reduce.3.cloned.1.call-done = f32[8,64,512]{2,1,0:T(8,128)} async-done(((f32[8,64,512]{2,1,0:T(8,128)}), f32[8,64,512]{2,1,0:T(8,128)}) %all-reduce.3.cloned.1.call-update) | async-done | bytes 1048592 | tf_op jit(solution)/shard_map/psum | solution.py:19
  67.6 2.0 fusion.4
  69.6 0.1 copy.24
  69.7 1.3 copy.21
  71.0 13.2 %scatter_custom_fusion = f32[64,4096]{0,1:T(8,128)} fusion(s32[2048]{0:T(1024)S(1)} %bitcast.33, f32[2048,64]{1,0:T(8,128)} %copy.21, f32[]{:T(128)} %constant.7.clone.1), kind=kCustom, calls=%fused_computation.7 | custom fusion | flops 131072 | bytes 1049088 | tf_op jit(solution)/shard_map/scatter-add | solution.py:27
  84.2 3.2 %copy.22 = f32[64,4096]{1,0:T(8,128)} copy(f32[64,4096]{0,1:T(8,128)} %scatter_custom_fusion) | data formatting | bytes 2097152 | tf_op jit(solution)/shard_map/scatter-add | solution.py:27
  87.4 0.0 reduce-scatter.2.cloned.1.call-update
  87.4 0.0 all-reduce.5.cloned.1.call-start
  87.5 26.7 %reduce-scatter.2.cloned.1.call-done = f32[64,1024]{1,0:T(8,128)} async-done(((f32[64,4096]{1,0:T(8,128)}), f32[64,1024]{1,0:T(8,128)}) %reduce-scatter.2.cloned.1.call-update) | async-done | bytes 262160 | tf_op jit(solution)/shard_map/reduce_scatter | solution.py:28
  114.2 0.0 all-reduce.5.cloned.1.call-update
  114.2 55.4 %all-reduce.5.cloned.1.call-done = f32[64,1024]{1,0:T(8,128)} async-done(((f32[64,1024]{1,0:T(8,128)}), f32[64,1024]{1,0:T(8,128)}) %all-reduce.5.cloned.1.call-update) | async-done | bytes 262160 | tf_op jit(solution)/shard_map/psum | solution.py:29
  169.6 1.0 subtract_convert_fusion
  170.6 0.9 stack.2
  171.5 4.6 %all-to-all-start = ((bf16[4,64,1024]{2,1,0:T(8,128)(2,1)}), bf16[4,64,1024]{2,1,0:T(8,128)(2,1)}, u32[]{:S(2)}, u32[]{:S(2)}) async-start(bf16[4,64,1024]{2,1,0:T(8,128)(2,1)} %stack.2), calls=%async_computation.1 | async-start | bytes 1048576 | tf_op jit(solution)/shard_map/all_to_all | solution.py:32
  176.1 0.9 fusion.11
  177.0 12.9 %all-to-all-done = bf16[4,64,1024]{2,1,0:T(8,128)(2,1)} async-done(((bf16[4,64,1024]{2,1,0:T(8,128)(2,1)}), bf16[4,64,1024]{2,1,0:T(8,128)(2,1)}, u32[]{:S(2)}, u32[]{:S(2)}) %all-to-all-start) | async-done | bytes 524320 | tf_op jit(solution)/shard_map/all_to_all | solution.py:32
  189.8 1.1 copy.25
  190.9 4.2 %convolution_convert_fusion = bf16[64,512]{1,0:T(8,128)(2,1)} fusion(bf16[64,4096]{1,0:T(8,128)(2,1)S(1)} %bitcast.31, bf16[512,4096]{1,0:T(8,128)(2,1)} %param.13), kind=kOutput, calls=%fused_computation.6 | convolution fusion | flops 268468224 | bytes 4784128 | tf_op jit(solution)/shard_map/dot_general | solution.py:34
  (9 shorter events, 0.0 us)
Async XLA Ops:
  7.2 60.5 %copy-start = (bf16[1,8,256,512]{3,2,1,0:T(8,128)(2,1)S(1)}, bf16[1,8,256,512]{3,2,1,0:T(8,128)(2,1)}, u32[]{:S(2)}) copy-start(bf16[1,8,256,512]{3,2,1,0:T(8,128)(2,1)} %param.9) | copy-start | bytes 6291460
  7.2 60.4 %all-reduce.3.cloned.1.call-start = ((), (), s32[]{:S(2)}) async-start(), calls=%async_computation.2 | async-start | bytes 2097152 | tf_op jit(solution)/shard_map/psum | solution.py:19
  12.8 101.3 %reduce-scatter.2.cloned.1.call-start = ((), (), s32[]{:S(2)}) async-start(), calls=%async_computation.3 | async-start | bytes 1310720 | tf_op jit(solution)/shard_map/reduce_scatter | solution.py:28
  84.2 85.4 %copy-start.2 = (bf16[64,1024]{1,0:T(8,128)(2,1)S(1)}, bf16[64,1024]{1,0:T(8,128)(2,1)}, u32[]{:S(2)}) copy-start(bf16[64,1024]{1,0:T(8,128)(2,1)} %param.12) | copy-start | bytes 393220
  87.4 88.6 %copy-start.1 = (f32[8,64,512]{2,1,0:T(8,128)S(1)}, f32[8,64,512]{2,1,0:T(8,128)}, u32[]{:S(2)}) copy-start(f32[8,64,512]{2,1,0:T(8,128)} %all-reduce.3.cloned.1.call-done) | copy-start | bytes 3145732
  87.4 82.2 %all-reduce.5.cloned.1.call-start = ((), (), s32[]{:S(2)}) async-start(), calls=%async_computation.4 | async-start | bytes 524288 | tf_op jit(solution)/shard_map/psum | solution.py:29
  171.5 18.4 %all-to-all-start = ((bf16[4,64,1024]{2,1,0:T(8,128)(2,1)}), bf16[4,64,1024]{2,1,0:T(8,128)(2,1)}, u32[]{:S(2)}, u32[]{:S(2)}) async-start(bf16[4,64,1024]{2,1,0:T(8,128)(2,1)} %stack.2), calls=%async_computation.1 | async-start | bytes 1048576 | tf_op jit(solution)/shard_map/all_to_all | solution.py:32
Sparse Core Ops, SparseCore 0:
  13.0 54.6 all-reduce.2
  87.6 26.5 reduce-scatter.1
  117.2 52.3 all-reduce.4
